TPU v7x, 32 devices: a whole 2x2x4 slice. The times are simulated.
32 devices in a mesh: tm: 8 (over z, x), mp: 4 (over y, core).
Axes of the slice: x: 2, y: 2, z: 4, core: 2. Of those that a mesh axis runs over, the one named last changes fastest.
Arguments:
- features: bfloat16 [256, 2048], P('tm'), may hold values from -6 to 6
- w_in: bfloat16 [2048, 4096], P(None, 'mp'), may hold values from -0.125 to 0.125
- b_in: float32 [4096], P('mp'), may hold values from -5 to 5
- output_weight: bfloat16 [4096, 256], P('mp'), may hold values from -0.09375 to 0.09375
- final_offset_entries: float32 [256], replicated, may hold values from -3 to 3
- transition: float32 [256, 256], replicated, may hold values from -1 to 1
- gains: float32 [256, 256], P('tm'), may hold values from 0 to 1
- smooth_gains: float32 [256, 256], P('tm'), may hold values from 0 to 1
Outputs:
- filtered: float32 [256, 256], P(('tm', 'mp'))
- smoothed: float32 [256, 256], P(('tm', 'mp'))
All inputs are finite; a program needn't handle non-finite values.
Results may differ from a plain program's by a relative error of at most 0.0021.
Values sent between devices are 32-bit elements; how exact they have to be, the bound alone decides.
A program may use at most 128 MiB of HBM per device.

v0:
```python
import jax
import jax.numpy as jnp
from jax import lax
from jax.sharding import PartitionSpec as P

HIGH = lax.Precision.HIGHEST


def passed_along(value, axis, steps):
    count = lax.axis_size(axis)
    initial, last = (max(0, -steps), min(count, count - steps))
    return lax.ppermute(value, axis, [(source, source + steps) for source in range(initial, last)])


def compose_diagonal(earlier, later):
    return (later[0] * earlier[0], later[0] * earlier[1] + later[1])


def sweep_up(mats, vecs):
    levels = [(mats, vecs)]
    while mats.shape[0] > 1:
        count = mats.shape[0]
        half = count // 2
        first_m = mats[0 : 2 * half : 2]
        second_m = mats[1 : 2 * half : 2]
        first_v = vecs[0 : 2 * half : 2]
        second_v = vecs[1 : 2 * half : 2]
        new_m = jnp.einsum("bij,bjk->bik", second_m, first_m, precision=HIGH)
        new_v = jnp.einsum("bij,bj->bi", second_m, first_v, precision=HIGH) + second_v
        mats, vecs = (new_m, new_v)
        levels.append((mats, vecs))
    return levels


def sweep_down(levels, incoming):
    states = incoming[None]
    for level in range(len(levels) - 2, -1, -1):
        mats, vecs = levels[level]
        count = mats.shape[0]
        half = count // 2
        evens = states
        odds = (
            jnp.einsum("bij,bj->bi", mats[0 : 2 * half : 2], evens, precision=HIGH)
            + vecs[0 : 2 * half : 2]
        )
        paired = jnp.stack([evens, odds], 1).reshape(2 * half, states.shape[1])
        states = paired
    return states


def carry_forward(block_m, block_v):
    grid = block_v.shape[0]

    def relay_time(step, incoming):
        outgoing = jnp.dot(block_m, incoming, precision=HIGH) + block_v
        return passed_along(outgoing, "tm", 1)

    return lax.fori_loop(0, lax.axis_size("tm") - 1, relay_time, jnp.zeros((grid,), jnp.float32))


def carry_backward(block_d, block_v):
    grid = block_v.shape[0]

    def relay_time(step, incoming):
        outgoing = block_d * incoming + block_v
        return passed_along(outgoing, "tm", -1)

    return lax.fori_loop(0, lax.axis_size("tm") - 1, relay_time, jnp.zeros((grid,), jnp.float32))


def on_device(
    features, w_in, b_in, output_weight, final_offset_entries, transition, gains, smooth_gains
):
    pre = jnp.dot(features, w_in, preferred_element_type=jnp.float32) + b_in
    hidden_layer = jax.nn.gelu(pre, approximate=True).astype(jnp.bfloat16)
    partial_measurement = jnp.dot(hidden_layer, output_weight, preferred_element_type=jnp.float32)
    share = features.shape[0] // lax.axis_size("mp")
    mp_place = lax.axis_index("mp")
    time_last = lax.axis_index("tm") == lax.axis_size("tm") - 1
    measured_values = lax.psum(partial_measurement, "mp") + final_offset_entries
    weight_here = smooth_gains
    forward_m = (1.0 - gains)[:, :, None] * transition[None]
    forward_variance = gains * measured_values
    levels = sweep_up(forward_m, forward_variance)
    incoming = carry_forward(levels[-1][0][0], levels[-1][1][0])
    before = sweep_down(levels, incoming)
    filtered = jnp.einsum("tij,tj->ti", forward_m, before, precision=HIGH) + forward_variance
    closing = jnp.where(time_last, 0.0, 1.0).astype(jnp.float32)
    weight_here = weight_here.at[-1].multiply(closing)
    predicted = jnp.dot(filtered, transition.T, precision=HIGH)
    backward_d = weight_here[::-1]
    backward_v = (filtered - weight_here * predicted)[::-1]
    prefix_d, prefix_v = lax.associative_scan(compose_diagonal, (backward_d, backward_v), axis=0)
    later_state = carry_backward(prefix_d[-1], prefix_v[-1])
    smoothed = (prefix_d * later_state[None] + prefix_v)[::-1]
    filtered = lax.dynamic_slice_in_dim(filtered, mp_place * share, share, 0)
    smoothed = lax.dynamic_slice_in_dim(smoothed, mp_place * share, share, 0)
    return (filtered, smoothed)


def solution(mesh):
    placed = (
        P("tm", None),
        P(None, "mp"),
        P("mp"),
        P("mp", None),
        P(),
        P(),
        P("tm", None),
        P("tm", None),
    )
    return jax.shard_map(
        on_device,
        mesh=mesh,
        in_specs=placed,
        out_specs=(P(("tm", "mp"), None), P(("tm", "mp"), None)),
        check_vma=False,
    )
```

profile of v0, /device:TPU:0, one launch (start us, length us, event | category | flops | bytes accessed | tf_op | source)
XLA Modules:
  0.0 162.2 jit_solution(11965233251702824456)
XLA Ops:
  1.7 3.2 %fusion.40 = f32[32,256]{1,0:T(8,128)S(1)} fusion(bf16[1024,256]{1,0:T(8,128)(2,1)S(1)} %copy-done, bf16[32,2048]{1,0:T(8,128)(2,1)} %param.14, bf16[2048,1024]{1,0:T(8,128)(2,1)} %param.15, f32[1024]{0:T(1024)} %param.16), kind=kOutput, calls=%fused_computation.49 | convolution fusion | flops 151322624 | bytes 4886528 | tf_op jit(solution)/shard_map/dot_general | solution.py:76
  4.9 12.9 %psum.7 = f32[32,256]{1,0:T(8,128)S(1)} all-reduce(f32[32,256]{1,0:T(8,128)S(1)} %fusion.40), channel_id=1, replica_groups=mesh['tm'=8,'mp'=4] {'mp'}, use_global_device_ids=true, to_apply=%region_0.0 | all-reduce | flops 8192 | bytes 65536 | tf_op jit(solution)/shard_map/psum | solution.py:80
  17.9 3.9 %broadcast_multiply_fusion = f32[32,256,256]{2,1,0:T(8,128)} fusion(f32[256,256]{1,0:T(8,128)S(1)} %copy-done.3, f32[32,256]{1,0:T(8,128)S(1)} %get-tuple-element.76), kind=kLoop, calls=%fused_computation.1 | loop fusion | flops 2097152 | bytes 8683520 | tf_op jit(solution)/shard_map/mul | solution.py:82
  21.8 5.8 %fusion.4 = f32[16,1,256]{2,1,0:T(1,128)S(1)} fusion(f32[32,256,256]{2,1,0:T(8,128)} %broadcast_multiply_fusion, f32[16,256,1]{1,0,2:T(8,128)S(1)} %bitcast.86), kind=kOutput, calls=%fused_computation.6 | convolution fusion | flops 12582912 | bytes 4227072 | tf_op jit(solution)/shard_map/bij,bj->bi/dot_general | solution.py:29
  27.6 8.5 %fusion.2 = f32[16,256,256]{2,1,0:T(8,128)S(1)} fusion(f32[32,256,256]{2,1,0:T(8,128)} %broadcast_multiply_fusion), kind=kOutput, calls=%fused_computation.4 | convolution fusion | flops 3221225472 | bytes 12582912 | tf_op jit(solution)/shard_map/bij,bjk->bik/dot_general | solution.py:28
  36.1 2.0 %copy-done.1 = f32[16,256,256]{2,1,0:T(8,128)} copy-done((f32[16,256,256]{2,1,0:T(8,128)}, f32[16,256,256]{2,1,0:T(8,128)S(1)}, u32[]{:S(2)}) %copy-start.1) | copy-done | bytes 4194328
  38.1 1.8 %fusion.12 = f32[8,1,256]{2,1,0:T(1,128)S(1)} fusion(f32[16,256,256]{2,1,0:T(8,128)S(1)} %fusion.2, f32[8,256,1]{1,0,2:T(8,128)S(1)} %bitcast.88), kind=kOutput, calls=%fused_computation.14 | convolution fusion | flops 6291456 | bytes 2113536 | tf_op jit(solution)/shard_map/bij,bj->bi/dot_general | solution.py:29
  40.0 4.3 %fusion.10 = f32[8,256,256]{2,1,0:T(8,128)S(1)} fusion(f32[16,256,256]{2,1,0:T(8,128)} %copy-done.1), kind=kOutput, calls=%fused_computation.12 | convolution fusion | flops 1610612736 | bytes 6291456 | tf_op jit(solution)/shard_map/bij,bjk->bik/dot_general | solution.py:28
  48.1 1.9 %fusion.26 = f32[2,256,256]{2,1,0:T(8,128)S(1)} fusion(f32[4,256,256]{2,1,0:T(8,128)} %copy-done.2), kind=kOutput, calls=%fused_computation.32 | convolution fusion | flops 402653184 | bytes 1572864 | tf_op jit(solution)/shard_map/bij,bjk->bik/dot_general | solution.py:28
  50.7 43.5 %while.21 = (s32[]{:T(128)}, f32[256]{0:T(256)S(1)}, f32[256,256]{1,0:T(8,128)S(1)}, f32[256]{0:T(256)S(1)}, s32[]{:T(128)}) while((s32[]{:T(128)}, f32[256]{0:T(256)S(1)}, f32[256,256]{1,0:T(8,128)S(1)}, f32[256]{0:T(256)S(1)}, s32[]{:T(128)}) %tuple.61), condition=%wide.region_2.0_spmd, body=%wide.region_1.0_spmd.sunk | while | flops 786690 | bytes 271461 | solution.py:58
  51.0 3.4 %collective-permute-start = (f32[256]{0:T(256)S(1)}, f32[256]{0:T(256)S(1)}, u32[]{:S(2)}, u32[]{:S(2)}) collective-permute-start(f32[256]{0:T(256)S(1)} %add.331), channel_id=1, source_target_pairs={{0,4},{4,8},{8,12},{12,16},{16,20},{20,24},{24,28},{1,5},{5,9},{9,... | collective-permute-start | bytes 3080 | tf_op jit(solution)/shard_map/while/body/eval_jaxpr/ppermute | solution.py:12
  56.0 4.2 %collective-permute-start = (f32[256]{0:T(256)S(1)}, f32[256]{0:T(256)S(1)}, u32[]{:S(2)}, u32[]{:S(2)}) collective-permute-start(f32[256]{0:T(256)S(1)} %add.331), channel_id=1, source_target_pairs={{0,4},{4,8},{8,12},{12,16},{16,20},{20,24},{24,28},{1,5},{5,9},{9,... | collective-permute-start | bytes 3080 | tf_op jit(solution)/shard_map/while/body/eval_jaxpr/ppermute | solution.py:12
  61.8 4.4 %collective-permute-start = (f32[256]{0:T(256)S(1)}, f32[256]{0:T(256)S(1)}, u32[]{:S(2)}, u32[]{:S(2)}) collective-permute-start(f32[256]{0:T(256)S(1)} %add.331), channel_id=1, source_target_pairs={{0,4},{4,8},{8,12},{12,16},{16,20},{20,24},{24,28},{1,5},{5,9},{9,... | collective-permute-start | bytes 3080 | tf_op jit(solution)/shard_map/while/body/eval_jaxpr/ppermute | solution.py:12
  67.7 5.1 %collective-permute-start = (f32[256]{0:T(256)S(1)}, f32[256]{0:T(256)S(1)}, u32[]{:S(2)}, u32[]{:S(2)}) collective-permute-start(f32[256]{0:T(256)S(1)} %add.331), channel_id=1, source_target_pairs={{0,4},{4,8},{8,12},{12,16},{16,20},{20,24},{24,28},{1,5},{5,9},{9,... | collective-permute-start | bytes 3080 | tf_op jit(solution)/shard_map/while/body/eval_jaxpr/ppermute | solution.py:12
  74.4 5.1 %collective-permute-start = (f32[256]{0:T(256)S(1)}, f32[256]{0:T(256)S(1)}, u32[]{:S(2)}, u32[]{:S(2)}) collective-permute-start(f32[256]{0:T(256)S(1)} %add.331), channel_id=1, source_target_pairs={{0,4},{4,8},{8,12},{12,16},{16,20},{20,24},{24,28},{1,5},{5,9},{9,... | collective-permute-start | bytes 3080 | tf_op jit(solution)/shard_map/while/body/eval_jaxpr/ppermute | solution.py:12
  81.1 5.1 %collective-permute-start = (f32[256]{0:T(256)S(1)}, f32[256]{0:T(256)S(1)}, u32[]{:S(2)}, u32[]{:S(2)}) collective-permute-start(f32[256]{0:T(256)S(1)} %add.331), channel_id=1, source_target_pairs={{0,4},{4,8},{8,12},{12,16},{16,20},{20,24},{24,28},{1,5},{5,9},{9,... | collective-permute-start | bytes 3080 | tf_op jit(solution)/shard_map/while/body/eval_jaxpr/ppermute | solution.py:12
  87.8 5.1 %collective-permute-start = (f32[256]{0:T(256)S(1)}, f32[256]{0:T(256)S(1)}, u32[]{:S(2)}, u32[]{:S(2)}) collective-permute-start(f32[256]{0:T(256)S(1)} %add.331), channel_id=1, source_target_pairs={{0,4},{4,8},{8,12},{12,16},{16,20},{20,24},{24,28},{1,5},{5,9},{9,... | collective-permute-start | bytes 3080 | tf_op jit(solution)/shard_map/while/body/eval_jaxpr/ppermute | solution.py:12
  94.6 1.6 %fusion.24 = f32[2,1,256]{2,1,0:T(1,128)S(1)} fusion(f32[4,256,256]{2,1,0:T(8,128)} %copy-done.2, f32[2,256,1]{1,0,2:T(2,128)S(1)} %get-tuple-element.101), kind=kOutput, calls=%fused_computation.30 | convolution fusion | flops 1572864 | bytes 528384 | tf_op jit(solution)/shard_map/bij,bj->bi/dot_general | solution.py:43
  97.3 3.4 %fusion.8 = f32[8,1,256]{2,1,0:T(1,128)S(1)} fusion(f32[8,256,1]{1,2,0:T(1,128)S(1)} %reshape.98, f32[16,256,256]{2,1,0:T(8,128)} %copy-done.1), kind=kOutput, calls=%fused_computation.10 | convolution fusion | flops 6291456 | bytes 2113536 | tf_op jit(solution)/shard_map/bij,bj->bi/dot_general | solution.py:43
  100.9 5.8 %fusion = f32[16,1,256]{2,1,0:T(1,128)S(1)} fusion(f32[16,256,1]{1,2,0:T(1,128)S(1)} %reshape.100, f32[32,256,256]{2,1,0:T(8,128)} %broadcast_multiply_fusion), kind=kOutput, calls=%fused_computation.2 | convolution fusion | flops 12582912 | bytes 4227072 | tf_op jit(solution)/shard_map/bij,bj->bi/dot_general | solution.py:43
  106.8 7.6 %fusion.7 = f32[32,1,256]{2,1,0:T(1,128)S(1)} fusion(f32[32,256,1]{1,2,0:T(1,128)S(1)} %reshape.102, f32[256,256]{1,0:T(8,128)S(1)} %copy-done.4, f32[32,256]{1,0:T(8,128)S(1)} %get-tuple-element.76), kind=kOutput, calls=%fused_computation.9 | convolution fusion | flops 27262976 | bytes 360448 | tf_op jit(solution)/shard_map/tij,tj->ti/dot_general | solution.py:87
  116.4 45.1 %while.22 = (s32[]{:T(128)}, f32[256]{0:T(256)S(1)}, f32[256]{0:T(256)S(1)}, f32[256]{0:T(256)S(1)}, s32[]{:T(128)}) while((s32[]{:T(128)}, f32[256]{0:T(256)S(1)}, f32[256]{0:T(256)S(1)}, f32[256]{0:T(256)S(1)}, s32[]{:T(128)}) %tuple.63), condition=%wide.region_4.5_spmd, body=%wide.region_3.4_spmd.sunk | while | flops 514 | bytes 8293 | solution.py:68
  116.4 1.3 collective-permute-start.1
  117.7 5.3 %collective-permute-done.1 = f32[256]{0:T(256)S(1)} collective-permute-done((f32[256]{0:T(256)S(1)}, f32[256]{0:T(256)S(1)}, u32[]{:S(2)}, u32[]{:S(2)}) %collective-permute-start.1) | collective-permute-done | bytes 1056 | tf_op jit(solution)/shard_map/while/body/eval_jaxpr/ppermute | solution.py:12
  124.3 5.3 %collective-permute-done.1 = f32[256]{0:T(256)S(1)} collective-permute-done((f32[256]{0:T(256)S(1)}, f32[256]{0:T(256)S(1)}, u32[]{:S(2)}, u32[]{:S(2)}) %collective-permute-start.1) | collective-permute-done | bytes 1056 | tf_op jit(solution)/shard_map/while/body/eval_jaxpr/ppermute | solution.py:12
  131.0 5.1 %collective-permute-done.1 = f32[256]{0:T(256)S(1)} collective-permute-done((f32[256]{0:T(256)S(1)}, f32[256]{0:T(256)S(1)}, u32[]{:S(2)}, u32[]{:S(2)}) %collective-permute-start.1) | collective-permute-done | bytes 1056 | tf_op jit(solution)/shard_map/while/body/eval_jaxpr/ppermute | solution.py:12
  136.0 1.3 collective-permute-start.1
  137.3 5.1 %collective-permute-done.1 = f32[256]{0:T(256)S(1)} collective-permute-done((f32[256]{0:T(256)S(1)}, f32[256]{0:T(256)S(1)}, u32[]{:S(2)}, u32[]{:S(2)}) %collective-permute-start.1) | collective-permute-done | bytes 1056 | tf_op jit(solution)/shard_map/while/body/eval_jaxpr/ppermute | solution.py:12
  143.7 5.1 %collective-permute-done.1 = f32[256]{0:T(256)S(1)} collective-permute-done((f32[256]{0:T(256)S(1)}, f32[256]{0:T(256)S(1)}, u32[]{:S(2)}, u32[]{:S(2)}) %collective-permute-start.1) | collective-permute-done | bytes 1056 | tf_op jit(solution)/shard_map/while/body/eval_jaxpr/ppermute | solution.py:12
  150.0 5.1 %collective-permute-done.1 = f32[256]{0:T(256)S(1)} collective-permute-done((f32[256]{0:T(256)S(1)}, f32[256]{0:T(256)S(1)}, u32[]{:S(2)}, u32[]{:S(2)}) %collective-permute-start.1) | collective-permute-done | bytes 1056 | tf_op jit(solution)/shard_map/while/body/eval_jaxpr/ppermute | solution.py:12
  155.1 1.3 collective-permute-start.1
  156.4 5.1 %collective-permute-done.1 = f32[256]{0:T(256)S(1)} collective-permute-done((f32[256]{0:T(256)S(1)}, f32[256]{0:T(256)S(1)}, u32[]{:S(2)}, u32[]{:S(2)}) %collective-permute-start.1) | collective-permute-done | bytes 1056 | tf_op jit(solution)/shard_map/while/body/eval_jaxpr/ppermute | solution.py:12
  (171 shorter events, 25.5 us)
Async XLA Ops:
  0.6 1.1 copy-start
  0.6 17.2 %copy-start.6 = (f32[256]{0:T(256)S(1)}, f32[256]{0:T(256)}, u32[]{:S(2)}) copy-start(f32[256]{0:T(256)} %param.18) | copy-start | bytes 3076
  0.7 17.2 %copy-start.5 = (f32[32,256]{1,0:T(8,128)S(1)}, f32[32,256]{1,0:T(8,128)}, u32[]{:S(2)}) copy-start(f32[32,256]{1,0:T(8,128)} %param.20) | copy-start | bytes 98308
  0.7 17.2 %copy-start.3 = (f32[256,256]{1,0:T(8,128)S(1)}, f32[256,256]{1,0:T(8,128)}, u32[]{:S(2)}) copy-start(f32[256,256]{1,0:T(8,128)} %param.19) | copy-start | bytes 786436
  36.1 2.0 %copy-start.1 = (f32[16,256,256]{2,1,0:T(8,128)}, f32[16,256,256]{2,1,0:T(8,128)S(1)}, u32[]{:S(2)}) copy-start(f32[16,256,256]{2,1,0:T(8,128)S(1)} %fusion.2) | copy-start | bytes 12582916
  46.5 1.0 copy-start.2
  51.0 4.7 %collective-permute-start = (f32[256]{0:T(256)S(1)}, f32[256]{0:T(256)S(1)}, u32[]{:S(2)}, u32[]{:S(2)}) collective-permute-start(f32[256]{0:T(256)S(1)} %add.331), channel_id=1, source_target_pairs={{0,4},{4,8},{8,12},{12,16},{16,20},{20,24},{24,28},{1,5},{5,9},{9,... | collective-permute-start | bytes 3080 | tf_op jit(solution)/shard_map/while/body/eval_jaxpr/ppermute | solution.py:12
  56.0 5.5 %collective-permute-start = (f32[256]{0:T(256)S(1)}, f32[256]{0:T(256)S(1)}, u32[]{:S(2)}, u32[]{:S(2)}) collective-permute-start(f32[256]{0:T(256)S(1)} %add.331), channel_id=1, source_target_pairs={{0,4},{4,8},{8,12},{12,16},{16,20},{20,24},{24,28},{1,5},{5,9},{9,... | collective-permute-start | bytes 3080 | tf_op jit(solution)/shard_map/while/body/eval_jaxpr/ppermute | solution.py:12
  61.8 5.7 %collective-permute-start = (f32[256]{0:T(256)S(1)}, f32[256]{0:T(256)S(1)}, u32[]{:S(2)}, u32[]{:S(2)}) collective-permute-start(f32[256]{0:T(256)S(1)} %add.331), channel_id=1, source_target_pairs={{0,4},{4,8},{8,12},{12,16},{16,20},{20,24},{24,28},{1,5},{5,9},{9,... | collective-permute-start | bytes 3080 | tf_op jit(solution)/shard_map/while/body/eval_jaxpr/ppermute | solution.py:12
  67.7 6.4 %collective-permute-start = (f32[256]{0:T(256)S(1)}, f32[256]{0:T(256)S(1)}, u32[]{:S(2)}, u32[]{:S(2)}) collective-permute-start(f32[256]{0:T(256)S(1)} %add.331), channel_id=1, source_target_pairs={{0,4},{4,8},{8,12},{12,16},{16,20},{20,24},{24,28},{1,5},{5,9},{9,... | collective-permute-start | bytes 3080 | tf_op jit(solution)/shard_map/while/body/eval_jaxpr/ppermute | solution.py:12
  74.4 6.4 %collective-permute-start = (f32[256]{0:T(256)S(1)}, f32[256]{0:T(256)S(1)}, u32[]{:S(2)}, u32[]{:S(2)}) collective-permute-start(f32[256]{0:T(256)S(1)} %add.331), channel_id=1, source_target_pairs={{0,4},{4,8},{8,12},{12,16},{16,20},{20,24},{24,28},{1,5},{5,9},{9,... | collective-permute-start | bytes 3080 | tf_op jit(solution)/shard_map/while/body/eval_jaxpr/ppermute | solution.py:12
  81.1 6.4 %collective-permute-start = (f32[256]{0:T(256)S(1)}, f32[256]{0:T(256)S(1)}, u32[]{:S(2)}, u32[]{:S(2)}) collective-permute-start(f32[256]{0:T(256)S(1)} %add.331), channel_id=1, source_target_pairs={{0,4},{4,8},{8,12},{12,16},{16,20},{20,24},{24,28},{1,5},{5,9},{9,... | collective-permute-start | bytes 3080 | tf_op jit(solution)/shard_map/while/body/eval_jaxpr/ppermute | solution.py:12
  87.8 6.4 %collective-permute-start = (f32[256]{0:T(256)S(1)}, f32[256]{0:T(256)S(1)}, u32[]{:S(2)}, u32[]{:S(2)}) collective-permute-start(f32[256]{0:T(256)S(1)} %add.331), channel_id=1, source_target_pairs={{0,4},{4,8},{8,12},{12,16},{16,20},{20,24},{24,28},{1,5},{5,9},{9,... | collective-permute-start | bytes 3080 | tf_op jit(solution)/shard_map/while/body/eval_jaxpr/ppermute | solution.py:12
  94.6 12.2 %copy-start.4 = (f32[256,256]{1,0:T(8,128)S(1)}, f32[256,256]{1,0:T(8,128)}, u32[]{:S(2)}) copy-start(f32[256,256]{1,0:T(8,128)} %param.19) | copy-start | bytes 786436
  116.4 6.6 %collective-permute-start.1 = (f32[256]{0:T(256)S(1)}, f32[256]{0:T(256)S(1)}, u32[]{:S(2)}, u32[]{:S(2)}) collective-permute-start(f32[256]{0:T(256)S(1)} %multiply_add_fusion.7), channel_id=1, source_target_pairs={{4,0},{8,4},{12,8},{16,12},{20,16},{24,20},{28,24},{5,1},{9,5},{13... | collective-permute-start | bytes 3080 | tf_op jit(solution)/shard_map/while/body/eval_jaxpr/ppermute | solution.py:12
  123.0 6.6 %collective-permute-start.1 = (f32[256]{0:T(256)S(1)}, f32[256]{0:T(256)S(1)}, u32[]{:S(2)}, u32[]{:S(2)}) collective-permute-start(f32[256]{0:T(256)S(1)} %multiply_add_fusion.7), channel_id=1, source_target_pairs={{4,0},{8,4},{12,8},{16,12},{20,16},{24,20},{28,24},{5,1},{9,5},{13... | collective-permute-start | bytes 3080 | tf_op jit(solution)/shard_map/while/body/eval_jaxpr/ppermute | solution.py:12
  129.7 6.4 %collective-permute-start.1 = (f32[256]{0:T(256)S(1)}, f32[256]{0:T(256)S(1)}, u32[]{:S(2)}, u32[]{:S(2)}) collective-permute-start(f32[256]{0:T(256)S(1)} %multiply_add_fusion.7), channel_id=1, source_target_pairs={{4,0},{8,4},{12,8},{16,12},{20,16},{24,20},{28,24},{5,1},{9,5},{13... | collective-permute-start | bytes 3080 | tf_op jit(solution)/shard_map/while/body/eval_jaxpr/ppermute | solution.py:12
  136.0 6.4 %collective-permute-start.1 = (f32[256]{0:T(256)S(1)}, f32[256]{0:T(256)S(1)}, u32[]{:S(2)}, u32[]{:S(2)}) collective-permute-start(f32[256]{0:T(256)S(1)} %multiply_add_fusion.7), channel_id=1, source_target_pairs={{4,0},{8,4},{12,8},{16,12},{20,16},{24,20},{28,24},{5,1},{9,5},{13... | collective-permute-start | bytes 3080 | tf_op jit(solution)/shard_map/while/body/eval_jaxpr/ppermute | solution.py:12
  142.4 6.4 %collective-permute-start.1 = (f32[256]{0:T(256)S(1)}, f32[256]{0:T(256)S(1)}, u32[]{:S(2)}, u32[]{:S(2)}) collective-permute-start(f32[256]{0:T(256)S(1)} %multiply_add_fusion.7), channel_id=1, source_target_pairs={{4,0},{8,4},{12,8},{16,12},{20,16},{24,20},{28,24},{5,1},{9,5},{13... | collective-permute-start | bytes 3080 | tf_op jit(solution)/shard_map/while/body/eval_jaxpr/ppermute | solution.py:12
  148.7 6.4 %collective-permute-start.1 = (f32[256]{0:T(256)S(1)}, f32[256]{0:T(256)S(1)}, u32[]{:S(2)}, u32[]{:S(2)}) collective-permute-start(f32[256]{0:T(256)S(1)} %multiply_add_fusion.7), channel_id=1, source_target_pairs={{4,0},{8,4},{12,8},{16,12},{20,16},{24,20},{28,24},{5,1},{9,5},{13... | collective-permute-start | bytes 3080 | tf_op jit(solution)/shard_map/while/body/eval_jaxpr/ppermute | solution.py:12
  155.1 6.4 %collective-permute-start.1 = (f32[256]{0:T(256)S(1)}, f32[256]{0:T(256)S(1)}, u32[]{:S(2)}, u32[]{:S(2)}) collective-permute-start(f32[256]{0:T(256)S(1)} %multiply_add_fusion.7), channel_id=1, source_target_pairs={{4,0},{8,4},{12,8},{16,12},{20,16},{24,20},{28,24},{5,1},{9,5},{13... | collective-permute-start | bytes 3080 | tf_op jit(solution)/shard_map/while/body/eval_jaxpr/ppermute | solution.py:12
where the time goes:
time: 163 us; the launch traced here: 162 us
  matrix products  50.8 us (31%)
  waiting for transfers between devices  44.9 us (28%)
  starting transfers between devices  41.5 us (25%)
  blocking collectives  12.9 us (8%)
  local copies, waits for them, and re-layouts  6.12 us (4%)
  other arithmetic  4.38 us (3%)
    ppermute x14, waiting for transfers between devices, passed_along(): lax.ppermute(value, axis, [(source, source + steps) for source in range(i...  44.9 us
    ppermute x14, starting transfers between devices, passed_along(): lax.ppermute(value, axis, [(source, source + steps) for source in range(i...  41.5 us
    dot_general x5, matrix products, sweep_up(): new_m = jnp.einsum('bij,bjk->bik', second_m, first_m, precision=HIGH)  16.2 us
    psum x1, blocking collectives, on_device(): measured_values = lax.psum(partial_measurement, 'mp') + final_offset_entries  12.9 us
    dot_general x5, matrix products, sweep_down(): jnp.einsum('bij,bj->bi', mats[0:2 * half:2], evens, precision=HIGH)  12.1 us
    dot_general x5, matrix products, sweep_up(): jnp.einsum('bij,bj->bi', second_m, first_v, precision=HIGH) + second_v  9.4 us
    dot_general x1, matrix products, on_device(): jnp.einsum('tij,tj->ti', forward_m, before, precision=HIGH)  7.61 us
    unnamed x15, local copies, waits for them, and re-layouts  4.02 us
  transfers between devices with their start and end apart: 14, of which 14 were waited for; matrix products, arithmetic and copies ran while one was open for 0% of the time, Pallas kernels for 0%

commit v1 on v0

--- a/solution.py
+++ b/solution.py
@@ -77,7 +77,9 @@
     share = features.shape[0] // lax.axis_size("mp")
     mp_place = lax.axis_index("mp")
     time_last = lax.axis_index("tm") == lax.axis_size("tm") - 1
-    measured_values = lax.psum(partial_measurement, "mp") + final_offset_entries
+    measured_values = (
+        jnp.sum(lax.all_gather(partial_measurement, "mp"), axis=0) + final_offset_entries
+    )
     weight_here = smooth_gains
     forward_m = (1.0 - gains)[:, :, None] * transition[None]
     forward_variance = gains * measured_values

time: 163 us -> 157 us (0.963)
  blocking collectives: 12.9 us -> 6.53 us
    psum x1 -> x0, blocking collectives: 12.9 us -> none  [on_device(): measured_values = lax.psum(partial_measurement, 'mp') + final_offset_entries]
    all_gather x0 -> x1, blocking collectives: none -> 6.53 us  [on_device(): lax.all_gather(partial_measurement, 'mp')]
where the time goes in v1:
time: 157 us; the launch traced here: 156 us
  matrix products  50.8 us (32%)
  waiting for transfers between devices  44.9 us (29%)
  starting transfers between devices  41.9 us (27%)
  blocking collectives  6.53 us (4%)
  local copies, waits for them, and re-layouts  6.12 us (4%)
  other arithmetic  4.39 us (3%)
    ppermute x14, waiting for transfers between devices, passed_along(): lax.ppermute(value, axis, [(source, source + steps) for source in range(i...  44.9 us
    ppermute x14, starting transfers between devices, passed_along(): lax.ppermute(value, axis, [(source, source + steps) for source in range(i...  41.9 us
    dot_general x5, matrix products, sweep_up(): new_m = jnp.einsum('bij,bjk->bik', second_m, first_m, precision=HIGH)  16.2 us
    dot_general x5, matrix products, sweep_down(): jnp.einsum('bij,bj->bi', mats[0:2 * half:2], evens, precision=HIGH)  12.1 us
    dot_general x5, matrix products, sweep_up(): jnp.einsum('bij,bj->bi', second_m, first_v, precision=HIGH) + second_v  9.4 us
    dot_general x1, matrix products, on_device(): jnp.einsum('tij,tj->ti', forward_m, before, precision=HIGH)  7.61 us
    all_gather x1, blocking collectives, on_device(): lax.all_gather(partial_measurement, 'mp')  6.53 us
    unnamed x15, local copies, waits for them, and re-layouts  4.02 us
  transfers between devices with their start and end apart: 14, of which 14 were waited for; matrix products, arithmetic and copies ran while one was open for 0% of the time, Pallas kernels for 0%

profile of v1, /device:TPU:0, one launch (start us, length us, event | category | flops | bytes accessed | tf_op | source)
XLA Modules:
  0.0 156.1 jit_solution(7917590339276007904)
XLA Ops:
  1.7 3.2 %fusion.40 = f32[32,256]{1,0:T(8,128)S(1)} fusion(bf16[1024,256]{1,0:T(8,128)(2,1)S(1)} %copy-done, bf16[32,2048]{1,0:T(8,128)(2,1)} %param.14, bf16[2048,1024]{1,0:T(8,128)(2,1)} %param.15, f32[1024]{0:T(1024)} %param.16), kind=kOutput, calls=%fused_computation.49 | convolution fusion | flops 151322624 | bytes 4886528 | tf_op jit(solution)/shard_map/dot_general | solution.py:76
  4.9 6.5 %all-gather = f32[128,256]{1,0:T(8,128)S(1)} all-gather(f32[32,256]{1,0:T(8,128)S(1)} %fusion.40), channel_id=2, replica_groups=mesh['tm'=8,'mp'=4] {'mp'}, dimensions={0}, use_global_device_ids=true | all-gather | bytes 163840 | tf_op jit(solution)/shard_map/all_gather | solution.py:81
  11.5 3.9 %broadcast_multiply_fusion = f32[32,256,256]{2,1,0:T(8,128)} fusion(f32[256,256]{1,0:T(8,128)S(1)} %copy-done.3, f32[32,256]{1,0:T(8,128)S(1)} %get-tuple-element.76), kind=kLoop, calls=%fused_computation.1 | loop fusion | flops 2097152 | bytes 8683520 | tf_op jit(solution)/shard_map/mul | solution.py:84
  15.4 5.8 %fusion.4 = f32[16,1,256]{2,1,0:T(1,128)S(1)} fusion(f32[32,256,256]{2,1,0:T(8,128)} %broadcast_multiply_fusion, f32[16,256,1]{1,0,2:T(8,128)S(1)} %bitcast.88), kind=kOutput, calls=%fused_computation.6 | convolution fusion | flops 12582912 | bytes 4227072 | tf_op jit(solution)/shard_map/bij,bj->bi/dot_general | solution.py:29
  21.2 8.5 %fusion.2 = f32[16,256,256]{2,1,0:T(8,128)S(1)} fusion(f32[32,256,256]{2,1,0:T(8,128)} %broadcast_multiply_fusion), kind=kOutput, calls=%fused_computation.4 | convolution fusion | flops 3221225472 | bytes 12582912 | tf_op jit(solution)/shard_map/bij,bjk->bik/dot_general | solution.py:28
  29.7 2.0 %copy-done.1 = f32[16,256,256]{2,1,0:T(8,128)} copy-done((f32[16,256,256]{2,1,0:T(8,128)}, f32[16,256,256]{2,1,0:T(8,128)S(1)}, u32[]{:S(2)}) %copy-start.1) | copy-done | bytes 4194328
  31.7 1.8 %fusion.12 = f32[8,1,256]{2,1,0:T(1,128)S(1)} fusion(f32[16,256,256]{2,1,0:T(8,128)S(1)} %fusion.2, f32[8,256,1]{1,0,2:T(8,128)S(1)} %bitcast.90), kind=kOutput, calls=%fused_computation.14 | convolution fusion | flops 6291456 | bytes 2113536 | tf_op jit(solution)/shard_map/bij,bj->bi/dot_general | solution.py:29
  33.6 4.3 %fusion.10 = f32[8,256,256]{2,1,0:T(8,128)S(1)} fusion(f32[16,256,256]{2,1,0:T(8,128)} %copy-done.1), kind=kOutput, calls=%fused_computation.12 | convolution fusion | flops 1610612736 | bytes 6291456 | tf_op jit(solution)/shard_map/bij,bjk->bik/dot_general | solution.py:28
  41.7 1.9 %fusion.26 = f32[2,256,256]{2,1,0:T(8,128)S(1)} fusion(f32[4,256,256]{2,1,0:T(8,128)} %copy-done.2), kind=kOutput, calls=%fused_computation.32 | convolution fusion | flops 402653184 | bytes 1572864 | tf_op jit(solution)/shard_map/bij,bjk->bik/dot_general | solution.py:28
  44.3 43.9 %while.21 = (s32[]{:T(128)}, f32[256]{0:T(256)S(1)}, f32[256,256]{1,0:T(8,128)S(1)}, f32[256]{0:T(256)S(1)}, s32[]{:T(128)}) while((s32[]{:T(128)}, f32[256]{0:T(256)S(1)}, f32[256,256]{1,0:T(8,128)S(1)}, f32[256]{0:T(256)S(1)}, s32[]{:T(128)}) %tuple.61), condition=%wide.region_2.0_spmd, body=%wide.region_1.0_spmd.sunk | while | flops 786690 | bytes 271461 | solution.py:58
  44.6 3.8 %collective-permute-start = (f32[256]{0:T(256)S(1)}, f32[256]{0:T(256)S(1)}, u32[]{:S(2)}, u32[]{:S(2)}) collective-permute-start(f32[256]{0:T(256)S(1)} %add.329), channel_id=1, source_target_pairs={{0,4},{4,8},{8,12},{12,16},{16,20},{20,24},{24,28},{1,5},{5,9},{9,... | collective-permute-start | bytes 3080 | tf_op jit(solution)/shard_map/while/body/eval_jaxpr/ppermute | solution.py:12
  50.0 4.2 %collective-permute-start = (f32[256]{0:T(256)S(1)}, f32[256]{0:T(256)S(1)}, u32[]{:S(2)}, u32[]{:S(2)}) collective-permute-start(f32[256]{0:T(256)S(1)} %add.329), channel_id=1, source_target_pairs={{0,4},{4,8},{8,12},{12,16},{16,20},{20,24},{24,28},{1,5},{5,9},{9,... | collective-permute-start | bytes 3080 | tf_op jit(solution)/shard_map/while/body/eval_jaxpr/ppermute | solution.py:12
  55.7 4.4 %collective-permute-start = (f32[256]{0:T(256)S(1)}, f32[256]{0:T(256)S(1)}, u32[]{:S(2)}, u32[]{:S(2)}) collective-permute-start(f32[256]{0:T(256)S(1)} %add.329), channel_id=1, source_target_pairs={{0,4},{4,8},{8,12},{12,16},{16,20},{20,24},{24,28},{1,5},{5,9},{9,... | collective-permute-start | bytes 3080 | tf_op jit(solution)/shard_map/while/body/eval_jaxpr/ppermute | solution.py:12
  61.7 5.1 %collective-permute-start = (f32[256]{0:T(256)S(1)}, f32[256]{0:T(256)S(1)}, u32[]{:S(2)}, u32[]{:S(2)}) collective-permute-start(f32[256]{0:T(256)S(1)} %add.329), channel_id=1, source_target_pairs={{0,4},{4,8},{8,12},{12,16},{16,20},{20,24},{24,28},{1,5},{5,9},{9,... | collective-permute-start | bytes 3080 | tf_op jit(solution)/shard_map/while/body/eval_jaxpr/ppermute | solution.py:12
  68.4 5.1 %collective-permute-start = (f32[256]{0:T(256)S(1)}, f32[256]{0:T(256)S(1)}, u32[]{:S(2)}, u32[]{:S(2)}) collective-permute-start(f32[256]{0:T(256)S(1)} %add.329), channel_id=1, source_target_pairs={{0,4},{4,8},{8,12},{12,16},{16,20},{20,24},{24,28},{1,5},{5,9},{9,... | collective-permute-start | bytes 3080 | tf_op jit(solution)/shard_map/while/body/eval_jaxpr/ppermute | solution.py:12
  75.1 5.1 %collective-permute-start = (f32[256]{0:T(256)S(1)}, f32[256]{0:T(256)S(1)}, u32[]{:S(2)}, u32[]{:S(2)}) collective-permute-start(f32[256]{0:T(256)S(1)} %add.329), channel_id=1, source_target_pairs={{0,4},{4,8},{8,12},{12,16},{16,20},{20,24},{24,28},{1,5},{5,9},{9,... | collective-permute-start | bytes 3080 | tf_op jit(solution)/shard_map/while/body/eval_jaxpr/ppermute | solution.py:12
  81.8 5.1 %collective-permute-start = (f32[256]{0:T(256)S(1)}, f32[256]{0:T(256)S(1)}, u32[]{:S(2)}, u32[]{:S(2)}) collective-permute-start(f32[256]{0:T(256)S(1)} %add.329), channel_id=1, source_target_pairs={{0,4},{4,8},{8,12},{12,16},{16,20},{20,24},{24,28},{1,5},{5,9},{9,... | collective-permute-start | bytes 3080 | tf_op jit(solution)/shard_map/while/body/eval_jaxpr/ppermute | solution.py:12
  88.6 1.6 %fusion.24 = f32[2,1,256]{2,1,0:T(1,128)S(1)} fusion(f32[4,256,256]{2,1,0:T(8,128)} %copy-done.2, f32[2,256,1]{1,0,2:T(2,128)S(1)} %get-tuple-element.101), kind=kOutput, calls=%fused_computation.30 | convolution fusion | flops 1572864 | bytes 528384 | tf_op jit(solution)/shard_map/bij,bj->bi/dot_general | solution.py:43
  91.3 3.4 %fusion.8 = f32[8,1,256]{2,1,0:T(1,128)S(1)} fusion(f32[8,256,1]{1,2,0:T(1,128)S(1)} %reshape.99, f32[16,256,256]{2,1,0:T(8,128)} %copy-done.1), kind=kOutput, calls=%fused_computation.10 | convolution fusion | flops 6291456 | bytes 2113536 | tf_op jit(solution)/shard_map/bij,bj->bi/dot_general | solution.py:43
  94.8 5.8 %fusion = f32[16,1,256]{2,1,0:T(1,128)S(1)} fusion(f32[16,256,1]{1,2,0:T(1,128)S(1)} %reshape.101, f32[32,256,256]{2,1,0:T(8,128)} %broadcast_multiply_fusion), kind=kOutput, calls=%fused_computation.2 | convolution fusion | flops 12582912 | bytes 4227072 | tf_op jit(solution)/shard_map/bij,bj->bi/dot_general | solution.py:43
  100.8 7.6 %fusion.7 = f32[32,1,256]{2,1,0:T(1,128)S(1)} fusion(f32[32,256,1]{1,2,0:T(1,128)S(1)} %reshape.103, f32[256,256]{1,0:T(8,128)S(1)} %copy-done.4, f32[32,256]{1,0:T(8,128)S(1)} %get-tuple-element.76), kind=kOutput, calls=%fused_computation.9 | convolution fusion | flops 27262976 | bytes 360448 | tf_op jit(solution)/shard_map/tij,tj->ti/dot_general | solution.py:89
  110.4 45.1 %while.22 = (s32[]{:T(128)}, f32[256]{0:T(256)S(1)}, f32[256]{0:T(256)S(1)}, f32[256]{0:T(256)S(1)}, s32[]{:T(128)}) while((s32[]{:T(128)}, f32[256]{0:T(256)S(1)}, f32[256]{0:T(256)S(1)}, f32[256]{0:T(256)S(1)}, s32[]{:T(128)}) %tuple.63), condition=%wide.region_4.5_spmd, body=%wide.region_3.4_spmd.sunk | while | flops 514 | bytes 8293 | solution.py:68
  110.4 1.3 collective-permute-start.1
  111.7 5.3 %collective-permute-done.1 = f32[256]{0:T(256)S(1)} collective-permute-done((f32[256]{0:T(256)S(1)}, f32[256]{0:T(256)S(1)}, u32[]{:S(2)}, u32[]{:S(2)}) %collective-permute-start.1) | collective-permute-done | bytes 1056 | tf_op jit(solution)/shard_map/while/body/eval_jaxpr/ppermute | solution.py:12
  117.0 1.3 collective-permute-start.1
  118.3 5.3 %collective-permute-done.1 = f32[256]{0:T(256)S(1)} collective-permute-done((f32[256]{0:T(256)S(1)}, f32[256]{0:T(256)S(1)}, u32[]{:S(2)}, u32[]{:S(2)}) %collective-permute-start.1) | collective-permute-done | bytes 1056 | tf_op jit(solution)/shard_map/while/body/eval_jaxpr/ppermute | solution.py:12
  123.6 1.3 collective-permute-start.1
  124.9 5.1 %collective-permute-done.1 = f32[256]{0:T(256)S(1)} collective-permute-done((f32[256]{0:T(256)S(1)}, f32[256]{0:T(256)S(1)}, u32[]{:S(2)}, u32[]{:S(2)}) %collective-permute-start.1) | collective-permute-done | bytes 1056 | tf_op jit(solution)/shard_map/while/body/eval_jaxpr/ppermute | solution.py:12
  131.3 5.1 %collective-permute-done.1 = f32[256]{0:T(256)S(1)} collective-permute-done((f32[256]{0:T(256)S(1)}, f32[256]{0:T(256)S(1)}, u32[]{:S(2)}, u32[]{:S(2)}) %collective-permute-start.1) | collective-permute-done | bytes 1056 | tf_op jit(solution)/shard_map/while/body/eval_jaxpr/ppermute | solution.py:12
  137.6 5.1 %collective-permute-done.1 = f32[256]{0:T(256)S(1)} collective-permute-done((f32[256]{0:T(256)S(1)}, f32[256]{0:T(256)S(1)}, u32[]{:S(2)}, u32[]{:S(2)}) %collective-permute-start.1) | collective-permute-done | bytes 1056 | tf_op jit(solution)/shard_map/while/body/eval_jaxpr/ppermute | solution.py:12
  144.0 5.1 %collective-permute-done.1 = f32[256]{0:T(256)S(1)} collective-permute-done((f32[256]{0:T(256)S(1)}, f32[256]{0:T(256)S(1)}, u32[]{:S(2)}, u32[]{:S(2)}) %collective-permute-start.1) | collective-permute-done | bytes 1056 | tf_op jit(solution)/shard_map/while/body/eval_jaxpr/ppermute | solution.py:12
  150.4 5.1 %collective-permute-done.1 = f32[256]{0:T(256)S(1)} collective-permute-done((f32[256]{0:T(256)S(1)}, f32[256]{0:T(256)S(1)}, u32[]{:S(2)}, u32[]{:S(2)}) %collective-permute-start.1) | collective-permute-done | bytes 1056 | tf_op jit(solution)/shard_map/while/body/eval_jaxpr/ppermute | solution.py:12
  (172 shorter events, 25.6 us)
Async XLA Ops:
  0.6 1.1 copy-start
  0.6 10.8 %copy-start.6 = (f32[256]{0:T(256)S(1)}, f32[256]{0:T(256)}, u32[]{:S(2)}) copy-start(f32[256]{0:T(256)} %param.18) | copy-start | bytes 3076
  0.7 10.8 %copy-start.5 = (f32[32,256]{1,0:T(8,128)S(1)}, f32[32,256]{1,0:T(8,128)}, u32[]{:S(2)}) copy-start(f32[32,256]{1,0:T(8,128)} %param.20) | copy-start | bytes 98308
  0.7 10.8 %copy-start.3 = (f32[256,256]{1,0:T(8,128)S(1)}, f32[256,256]{1,0:T(8,128)}, u32[]{:S(2)}) copy-start(f32[256,256]{1,0:T(8,128)} %param.19) | copy-start | bytes 786436
  29.7 2.0 %copy-start.1 = (f32[16,256,256]{2,1,0:T(8,128)}, f32[16,256,256]{2,1,0:T(8,128)S(1)}, u32[]{:S(2)}) copy-start(f32[16,256,256]{2,1,0:T(8,128)S(1)} %fusion.2) | copy-start | bytes 12582916
  40.1 1.0 copy-start.2
  44.6 5.1 %collective-permute-start = (f32[256]{0:T(256)S(1)}, f32[256]{0:T(256)S(1)}, u32[]{:S(2)}, u32[]{:S(2)}) collective-permute-start(f32[256]{0:T(256)S(1)} %add.329), channel_id=1, source_target_pairs={{0,4},{4,8},{8,12},{12,16},{16,20},{20,24},{24,28},{1,5},{5,9},{9,... | collective-permute-start | bytes 3080 | tf_op jit(solution)/shard_map/while/body/eval_jaxpr/ppermute | solution.py:12
  50.0 5.5 %collective-permute-start = (f32[256]{0:T(256)S(1)}, f32[256]{0:T(256)S(1)}, u32[]{:S(2)}, u32[]{:S(2)}) collective-permute-start(f32[256]{0:T(256)S(1)} %add.329), channel_id=1, source_target_pairs={{0,4},{4,8},{8,12},{12,16},{16,20},{20,24},{24,28},{1,5},{5,9},{9,... | collective-permute-start | bytes 3080 | tf_op jit(solution)/shard_map/while/body/eval_jaxpr/ppermute | solution.py:12
  55.7 5.7 %collective-permute-start = (f32[256]{0:T(256)S(1)}, f32[256]{0:T(256)S(1)}, u32[]{:S(2)}, u32[]{:S(2)}) collective-permute-start(f32[256]{0:T(256)S(1)} %add.329), channel_id=1, source_target_pairs={{0,4},{4,8},{8,12},{12,16},{16,20},{20,24},{24,28},{1,5},{5,9},{9,... | collective-permute-start | bytes 3080 | tf_op jit(solution)/shard_map/while/body/eval_jaxpr/ppermute | solution.py:12
  61.7 6.4 %collective-permute-start = (f32[256]{0:T(256)S(1)}, f32[256]{0:T(256)S(1)}, u32[]{:S(2)}, u32[]{:S(2)}) collective-permute-start(f32[256]{0:T(256)S(1)} %add.329), channel_id=1, source_target_pairs={{0,4},{4,8},{8,12},{12,16},{16,20},{20,24},{24,28},{1,5},{5,9},{9,... | collective-permute-start | bytes 3080 | tf_op jit(solution)/shard_map/while/body/eval_jaxpr/ppermute | solution.py:12
  68.4 6.4 %collective-permute-start = (f32[256]{0:T(256)S(1)}, f32[256]{0:T(256)S(1)}, u32[]{:S(2)}, u32[]{:S(2)}) collective-permute-start(f32[256]{0:T(256)S(1)} %add.329), channel_id=1, source_target_pairs={{0,4},{4,8},{8,12},{12,16},{16,20},{20,24},{24,28},{1,5},{5,9},{9,... | collective-permute-start | bytes 3080 | tf_op jit(solution)/shard_map/while/body/eval_jaxpr/ppermute | solution.py:12
  75.1 6.4 %collective-permute-start = (f32[256]{0:T(256)S(1)}, f32[256]{0:T(256)S(1)}, u32[]{:S(2)}, u32[]{:S(2)}) collective-permute-start(f32[256]{0:T(256)S(1)} %add.329), channel_id=1, source_target_pairs={{0,4},{4,8},{8,12},{12,16},{16,20},{20,24},{24,28},{1,5},{5,9},{9,... | collective-permute-start | bytes 3080 | tf_op jit(solution)/shard_map/while/body/eval_jaxpr/ppermute | solution.py:12
  81.8 6.4 %collective-permute-start = (f32[256]{0:T(256)S(1)}, f32[256]{0:T(256)S(1)}, u32[]{:S(2)}, u32[]{:S(2)}) collective-permute-start(f32[256]{0:T(256)S(1)} %add.329), channel_id=1, source_target_pairs={{0,4},{4,8},{8,12},{12,16},{16,20},{20,24},{24,28},{1,5},{5,9},{9,... | collective-permute-start | bytes 3080 | tf_op jit(solution)/shard_map/while/body/eval_jaxpr/ppermute | solution.py:12
  88.5 12.2 %copy-start.4 = (f32[256,256]{1,0:T(8,128)S(1)}, f32[256,256]{1,0:T(8,128)}, u32[]{:S(2)}) copy-start(f32[256,256]{1,0:T(8,128)} %param.19) | copy-start | bytes 786436
  110.4 6.6 %collective-permute-start.1 = (f32[256]{0:T(256)S(1)}, f32[256]{0:T(256)S(1)}, u32[]{:S(2)}, u32[]{:S(2)}) collective-permute-start(f32[256]{0:T(256)S(1)} %multiply_add_fusion.7), channel_id=1, source_target_pairs={{4,0},{8,4},{12,8},{16,12},{20,16},{24,20},{28,24},{5,1},{9,5},{13... | collective-permute-start | bytes 3080 | tf_op jit(solution)/shard_map/while/body/eval_jaxpr/ppermute | solution.py:12
  117.0 6.6 %collective-permute-start.1 = (f32[256]{0:T(256)S(1)}, f32[256]{0:T(256)S(1)}, u32[]{:S(2)}, u32[]{:S(2)}) collective-permute-start(f32[256]{0:T(256)S(1)} %multiply_add_fusion.7), channel_id=1, source_target_pairs={{4,0},{8,4},{12,8},{16,12},{20,16},{24,20},{28,24},{5,1},{9,5},{13... | collective-permute-start | bytes 3080 | tf_op jit(solution)/shard_map/while/body/eval_jaxpr/ppermute | solution.py:12
  123.6 6.4 %collective-permute-start.1 = (f32[256]{0:T(256)S(1)}, f32[256]{0:T(256)S(1)}, u32[]{:S(2)}, u32[]{:S(2)}) collective-permute-start(f32[256]{0:T(256)S(1)} %multiply_add_fusion.7), channel_id=1, source_target_pairs={{4,0},{8,4},{12,8},{16,12},{20,16},{24,20},{28,24},{5,1},{9,5},{13... | collective-permute-start | bytes 3080 | tf_op jit(solution)/shard_map/while/body/eval_jaxpr/ppermute | solution.py:12
  130.0 6.4 %collective-permute-start.1 = (f32[256]{0:T(256)S(1)}, f32[256]{0:T(256)S(1)}, u32[]{:S(2)}, u32[]{:S(2)}) collective-permute-start(f32[256]{0:T(256)S(1)} %multiply_add_fusion.7), channel_id=1, source_target_pairs={{4,0},{8,4},{12,8},{16,12},{20,16},{24,20},{28,24},{5,1},{9,5},{13... | collective-permute-start | bytes 3080 | tf_op jit(solution)/shard_map/while/body/eval_jaxpr/ppermute | solution.py:12
  136.4 6.4 %collective-permute-start.1 = (f32[256]{0:T(256)S(1)}, f32[256]{0:T(256)S(1)}, u32[]{:S(2)}, u32[]{:S(2)}) collective-permute-start(f32[256]{0:T(256)S(1)} %multiply_add_fusion.7), channel_id=1, source_target_pairs={{4,0},{8,4},{12,8},{16,12},{20,16},{24,20},{28,24},{5,1},{9,5},{13... | collective-permute-start | bytes 3080 | tf_op jit(solution)/shard_map/while/body/eval_jaxpr/ppermute | solution.py:12
  142.7 6.4 %collective-permute-start.1 = (f32[256]{0:T(256)S(1)}, f32[256]{0:T(256)S(1)}, u32[]{:S(2)}, u32[]{:S(2)}) collective-permute-start(f32[256]{0:T(256)S(1)} %multiply_add_fusion.7), channel_id=1, source_target_pairs={{4,0},{8,4},{12,8},{16,12},{20,16},{24,20},{28,24},{5,1},{9,5},{13... | collective-permute-start | bytes 3080 | tf_op jit(solution)/shard_map/while/body/eval_jaxpr/ppermute | solution.py:12
  149.1 6.4 %collective-permute-start.1 = (f32[256]{0:T(256)S(1)}, f32[256]{0:T(256)S(1)}, u32[]{:S(2)}, u32[]{:S(2)}) collective-permute-start(f32[256]{0:T(256)S(1)} %multiply_add_fusion.7), channel_id=1, source_target_pairs={{4,0},{8,4},{12,8},{16,12},{20,16},{24,20},{28,24},{5,1},{9,5},{13... | collective-permute-start | bytes 3080 | tf_op jit(solution)/shard_map/while/body/eval_jaxpr/ppermute | solution.py:12
